TPU v7x, 32 devices: a 4x2x2 block of a 4x4x8 slice. The times are simulated.
32 devices in a mesh: dp: 4 (over y, z), tp: 8 (over x, core).
Axes of the slice: x: 4, y: 2, z: 2, core: 2. Of those that a mesh axis runs over, the one named last changes fastest.
The devices are a block of a 4x4x8 slice.
Arguments:
- x_in: bfloat16 [2304, 4096], P(('dp', 'tp')), parts along dimension 0
- req_ids: int32 [2304], P('dp'), parts along dimension 0
- positions: int32 [2304], P('dp'), parts along dimension 0
- block_table: int32 [260, 64], P('dp'), parts along dimension 0
- ctx_len: int32 [260], P('dp'), parts along dimension 0
- k_pages: bfloat16 [4352, 16, 8, 128], P('dp', None, 'tp'), parts along dimension 0
- v_pages: bfloat16 [4352, 16, 8, 128], P('dp', None, 'tp'), parts along dimension 0
- w_q: bfloat16 [4096, 4096], P(None, 'tp')
- w_k: bfloat16 [4096, 1024], P(None, 'tp')
- w_v: bfloat16 [4096, 1024], P(None, 'tp')
- w_o: bfloat16 [4096, 4096], P('tp')
- w_gate: bfloat16 [4096, 14336], P(None, 'tp')
- w_up: bfloat16 [4096, 14336], P(None, 'tp')
- w_down: bfloat16 [14336, 4096], P('tp')
- g_attn: bfloat16 [4096], replicated
- g_mlp: bfloat16 [4096], replicated
Outputs:
- output 1: bfloat16 [2304, 4096], P(('dp', 'tp')), parts along dimension 0
- output 2: bfloat16 [4352, 16, 8, 128], P('dp', None, 'tp'), parts along dimension 0
- output 3: bfloat16 [4352, 16, 8, 128], P('dp', None, 'tp'), parts along dimension 0
There are 4 independent parts. A program takes and returns all parts, laid end to end along the dimension named above; an argument that names none is the same for every part.
All inputs are finite; a program needn't handle non-finite values.
Results may differ from a plain program's by a relative error of at most 0.017261.
Values are sent between devices in bfloat16 or wider.
A program may use at most 768 MiB of HBM per device.

v0:
```python
import jax
import jax.numpy as jnp
from jax import lax
from jax.sharding import PartitionSpec as P, NamedSharding

EPS = 1e-5
THETA = 500000.0


def rms_norm(rows, gain):
    rows32 = rows.astype(jnp.float32)
    inv_rms = lax.rsqrt(jnp.mean(rows32 * rows32, axis=-1, keepdims=True) + EPS)
    return (rows32 * inv_rms * gain.astype(jnp.float32)).astype(jnp.bfloat16)


def rotary(vals, positions):
    half_dim = vals.shape[-1] // 2
    inv_freq = THETA ** (-jnp.arange(half_dim, dtype=jnp.float32) * 2.0 / vals.shape[-1])
    angles = positions.astype(jnp.float32)[:, None] * inv_freq[None, :]
    cosine = jnp.cos(angles)[:, None, :]
    sine_val = jnp.sin(angles)[:, None, :]
    vals32 = vals.astype(jnp.float32)
    first_half = vals32[..., :half_dim]
    second_half = vals32[..., half_dim:]
    return jnp.concatenate([first_half * cosine - second_half * sine_val, second_half * cosine + first_half * sine_val], axis=-1).astype(jnp.bfloat16)


def softmax_mix(scores, key_mask, form, values):
    scores = jnp.where(key_mask, scores, -1e30)
    row_max = jnp.max(scores, axis=-1, keepdims=True)
    weights = jnp.exp(scores - row_max)
    weight_sum = jnp.sum(weights, axis=-1, keepdims=True)
    mixed_out = jnp.einsum(form, weights.astype(jnp.bfloat16), values, preferred_element_type=jnp.float32)
    return (mixed_out / weight_sum).astype(jnp.bfloat16)


def qkv_cache(hidden, positions, req_ids, block_table, k_pages, v_pages, w_q, w_k, w_v):
    tokens = hidden.shape[0]
    head_dim = k_pages.shape[3]
    page_len = k_pages.shape[1]
    q_rows = jnp.dot(hidden, w_q, preferred_element_type=jnp.float32).astype(jnp.bfloat16).reshape(tokens, -1, head_dim)
    k_rows = jnp.dot(hidden, w_k, preferred_element_type=jnp.float32).astype(jnp.bfloat16).reshape(tokens, -1, head_dim)
    v_rows = jnp.dot(hidden, w_v, preferred_element_type=jnp.float32).astype(jnp.bfloat16).reshape(tokens, -1, head_dim)
    q_rows = rotary(q_rows, positions)
    k_rows = rotary(k_rows, positions)
    page_ids = block_table[req_ids, positions // page_len]
    slot_ids = positions % page_len
    k_cache = k_pages.at[page_ids, slot_ids].set(k_rows)
    v_cache = v_pages.at[page_ids, slot_ids].set(v_rows)
    return q_rows, k_cache, v_cache


def attend(q_rows, k_cache, v_cache, req_ids, positions, block_table, ctx_len):
    tokens, n_heads, head_dim = q_rows.shape
    kv_heads = k_cache.shape[2]
    group_rep = n_heads // kv_heads
    decode_len = block_table.shape[0] - 1
    chunk_len = tokens - decode_len
    key_span = block_table.shape[1] * k_cache.shape[1]
    attn_scale = head_dim ** -0.5
    last_key = jnp.minimum(positions, ctx_len[req_ids] - 1)
    key_pos = jnp.arange(key_span)
    chunk_row = lax.dynamic_index_in_dim(block_table, req_ids[0], axis=0, keepdims=False)
    chunk_keys = k_cache[chunk_row].reshape(key_span, kv_heads, head_dim)
    chunk_vals = v_cache[chunk_row].reshape(key_span, kv_heads, head_dim)
    chunk_q = q_rows[:chunk_len].reshape(chunk_len, kv_heads, group_rep, head_dim)
    chunk_scores = jnp.einsum('cgrd,tgd->gcrt', chunk_q, chunk_keys, preferred_element_type=jnp.float32) * attn_scale
    chunk_mask = (key_pos[None, :] <= last_key[:chunk_len, None])[None, :, None, :]
    chunk_out = softmax_mix(chunk_scores, chunk_mask, 'gcrt,tgd->gcrd', chunk_vals)
    chunk_out = jnp.transpose(chunk_out, (1, 0, 2, 3)).reshape(chunk_len, n_heads * head_dim)
    dec_rows = block_table[req_ids[chunk_len:]]
    dec_keys = k_cache[dec_rows].reshape(decode_len, key_span, kv_heads, head_dim)
    dec_vals = v_cache[dec_rows].reshape(decode_len, key_span, kv_heads, head_dim)
    dec_q = q_rows[chunk_len:].reshape(decode_len, kv_heads, group_rep, head_dim)
    dec_scores = jnp.einsum('ngrd,ntgd->ngrt', dec_q, dec_keys, preferred_element_type=jnp.float32) * attn_scale
    dec_mask = (key_pos[None, :] <= last_key[chunk_len:, None])[:, None, None, :]
    dec_out = softmax_mix(dec_scores, dec_mask, 'ngrt,ntgd->ngrd', dec_vals).reshape(decode_len, n_heads * head_dim)
    return jnp.concatenate([chunk_out, dec_out], axis=0)


def solution(mesh):
    row_spec = P(('dp', 'tp'), None)
    group_vec = P('dp')
    table_spec = P('dp', None)
    cache_spec = P('dp', None, 'tp', None)
    col_split = P(None, 'tp')
    row_split = P('tp', None)
    gain_spec = P(None)

    def device_layer(x_in, req_ids, positions, block_table, ctx_len, k_pages, v_pages, w_q, w_k, w_v, w_o, w_gate, w_up, w_down, g_attn, g_mlp):
        hidden = lax.all_gather(rms_norm(x_in, g_attn), 'tp', axis=0, tiled=True)
        q_rows, k_cache, v_cache = qkv_cache(hidden, positions, req_ids, block_table, k_pages, v_pages, w_q, w_k, w_v)
        attn_rows = attend(q_rows, k_cache, v_cache, req_ids, positions, block_table, ctx_len)
        attn_part = jnp.dot(attn_rows, w_o, preferred_element_type=jnp.float32).astype(jnp.bfloat16)
        attn_sum = lax.psum_scatter(attn_part, 'tp', scatter_dimension=0, tiled=True)
        mid_rows = (x_in.astype(jnp.float32) + attn_sum.astype(jnp.float32)).astype(jnp.bfloat16)
        hidden_mlp = lax.all_gather(rms_norm(mid_rows, g_mlp), 'tp', axis=0, tiled=True)
        gate_proj = jnp.dot(hidden_mlp, w_gate, preferred_element_type=jnp.float32)
        up_proj = jnp.dot(hidden_mlp, w_up, preferred_element_type=jnp.float32)
        act_rows = (jax.nn.silu(gate_proj) * up_proj).astype(jnp.bfloat16)
        down_part = jnp.dot(act_rows, w_down, preferred_element_type=jnp.float32).astype(jnp.bfloat16)
        down_sum = lax.psum_scatter(down_part, 'tp', scatter_dimension=0, tiled=True)
        x_out = (mid_rows.astype(jnp.float32) + down_sum.astype(jnp.float32)).astype(jnp.bfloat16)
        return x_out, k_cache, v_cache

    return jax.shard_map(device_layer, mesh=mesh, in_specs=(row_spec, group_vec, group_vec, table_spec, group_vec, cache_spec, cache_spec, col_split, col_split, col_split, row_split, col_split, col_split, row_split, gain_spec, gain_spec), out_specs=(row_spec, cache_spec, cache_spec), check_vma=False)
```

profile of v0, /device:TPU:80, one launch (start us, length us, event | category | flops | bytes accessed | tf_op | source)
XLA Modules:
  0.0 469.0 jit_solution(13632055627019077731)
XLA Ops:
  7.3 4.4 copy.65
  12.3 2.1 copy.66
  14.7 1.0 fusion.11
  16.5 3.8 gather_fusion
  20.4 4.0 gather_fusion.1
  27.8 2.0 multiply_cosine_fusion
  29.8 19.8 %all-gather.3.cloned.1.call-done = bf16[576,4096]{1,0:T(8,128)(2,1)} async-done(((bf16[72,4096]{1,0:T(8,128)(2,1)}), bf16[576,4096]{1,0:T(8,128)(2,1)}) %all-gather.3.cloned.1.call-update) | async-done | bytes 4718608 | tf_op jit(solution)/shard_map/all_gather | solution.py:91
  49.6 4.0 fusion.18
  53.6 0.7 fusion.37
  54.5 67.0 %scatter_fusion = bf16[1088,16,128]{2,1,0:T(8,128)(2,1)} fusion(bf16[1088,16,128]{2,1,0:T(8,128)(2,1)} %bitcast.50, s32[576]{0:T(1024)S(1)} %fusion.47, bf16[576,128]{1,0:T(8,128)(2,1)S(1)} %copy.41), kind=kCustom, calls=%fused_computation.7 | custom fusion | bytes 446976 | tf_op jit(solution)/shard_map/scatter | solution.py:48
  121.5 3.6 gather_fusion.2
  125.1 3.7 convolution_convert_fusion.4
  128.8 67.0 %scatter_fusion.1 = bf16[1088,16,128]{2,1,0:T(8,128)(2,1)} fusion(bf16[1088,16,128]{2,1,0:T(8,128)(2,1)} %bitcast.48, s32[576]{0:T(1024)S(1)} %fusion.47, bf16[576,128]{1,0:T(8,128)(2,1)S(1)} %convolution_convert_fusion.4), kind=kCustom, calls=%fused_computation.8 | custom fusion | bytes 446976 | tf_op jit(solution)/shard_map/scatter | solution.py:49
  195.9 3.6 gather_fusion.3
  199.5 34.2 %gather_fusion.5 = bf16[4096,16,128]{2,1,0:T(8,128)(2,1)} fusion(bf16[1088,16,128]{2,1,0:T(8,128)(2,1)} %scatter_fusion, s32[4096]{0:T(1024)S(1)} %broadcast_clamp_fusion), kind=kCustom, calls=%fused_computation.5 | custom fusion | bytes 33570816 | tf_op jit(solution)/shard_map/gather | solution.py:72
  233.6 34.2 %gather_fusion.6 = bf16[4096,16,128]{2,1,0:T(8,128)(2,1)} fusion(bf16[1088,16,128]{2,1,0:T(8,128)(2,1)} %scatter_fusion.1, s32[4096]{0:T(1024)S(1)} %broadcast_clamp_fusion), kind=kCustom, calls=%fused_computation.6 | custom fusion | bytes 33570816 | tf_op jit(solution)/shard_map/gather | solution.py:73
  267.8 7.2 %fusion.8 = f32[576,512]{1,0:T(8,128)} fusion(bf16[576,4096]{1,0:T(8,128)(2,1)} %all-gather.3.cloned.1.call-done, bf16[4096,512]{1,0:T(8,128)(2,1)} %param.23), kind=kOutput, calls=%fused_computation.30 | convolution fusion | flops 2416508928 | bytes 10092544 | tf_op jit(solution)/shard_map/dot_general | solution.py:41
  275.0 1.9 reshape.330
  278.1 10.3 %fusion.55 = (f32[64,4]{1,0:T(8,128)S(1)}, f32[64,4,1024]{2,1,0:T(4,128)S(1)}) fusion(bf16[64,1024,128]{2,1,0:T(8,128)(2,1)} %bitcast.53, bf16[64,4,128]{2,0,1:T(8,128)(2,1)S(1)} %pad_maximum_fusion, pred[64,1024]{1,0:T(8,128)(4,1)S(1)} %iota_compare_fusion.1), kind=kOutput, calls=%fused_computation.114 | convolution fusion | flops 67895040 | bytes 17957888 | tf_op jit(solution)/shard_map/ngrd,ntgd->ngrt/dot_general | solution.py:75
  288.9 7.2 %fusion.19 = bf16[64,4,128]{2,1,0:T(4,128)(2,1)S(1)} fusion(bf16[64,1024,128]{2,1,0:T(8,128)(2,1)} %bitcast.52, f32[64,4,1024]{2,1,0:T(4,128)S(1)} %get-tuple-element.19, f32[64,4]{1,0:T(8,128)S(1)} %get-tuple-element.18, f32[64,4]{1,0:T(8,128)S(1)} %fusion.22), kind=kOutput, calls=%fused_computation.46 | convolution fusion | flops 67698688 | bytes 17893376 | tf_op jit(solution)/shard_map/ngrt,ntgd->ngrd/dot_general | solution.py:33
  296.2 3.0 fusion
  299.2 2.5 fusion.1
  301.7 2.5 divide_convert_fusion
  304.2 4.4 convolution_convert_fusion
  309.3 35.5 %reduce-scatter.3.cloned.1.call-done = bf16[72,4096]{1,0:T(8,128)(2,1)} async-done(((bf16[576,4096]{1,0:T(8,128)(2,1)}), bf16[72,4096]{1,0:T(8,128)(2,1)}) %reduce-scatter.3.cloned.1.call-update) | async-done | bytes 589840 | tf_op jit(solution)/shard_map/reduce_scatter | solution.py:95
  344.8 1.4 fusion.13
  346.2 2.1 fusion.15
  348.5 29.9 %all-gather.5.cloned.1.call-done = bf16[576,4096]{1,0:T(8,128)(2,1)} async-done(((bf16[72,4096]{1,0:T(8,128)(2,1)}), bf16[576,4096]{1,0:T(8,128)(2,1)}) %all-gather.5.cloned.1.call-update) | async-done | bytes 4718608 | tf_op jit(solution)/shard_map/all_gather | solution.py:97
  378.5 14.7 %fusion.56 = f32[576,1792]{1,0:T(8,128)} fusion(bf16[576,4096]{1,0:T(8,128)(2,1)} %all-gather.5.cloned.1.call-done, bf16[4096,1792]{1,0:T(8,128)(2,1)} %param.27), kind=kOutput, calls=%fused_computation.115 | convolution fusion | flops 8455716864 | bytes 23527424 | tf_op jit(solution)/shard_map/dot_general | solution.py:98
  393.2 30.9 %convolution_convert_fusion.1 = bf16[576,4096]{1,0:T(8,128)(2,1)} fusion(bf16[1792,4096]{1,0:T(8,128)(2,1)} %param.29, f32[576,1792]{1,0:T(8,128)} %fusion.56, bf16[576,4096]{1,0:T(8,128)(2,1)} %all-gather.5.cloned.1.call-done, bf16[4096,1792]{1,0:T(8,128)(2,1)} %param.28), kind=kOutput, calls=%fused_computation.15 | convolution fusion | flops 16919986176 | bytes 42926080 | tf_op jit(solution)/shard_map/dot_general | solution.py:101
  424.1 36.2 %reduce-scatter.5.cloned.1.call-done = bf16[72,4096]{1,0:T(8,128)(2,1)} async-done(((bf16[576,4096]{1,0:T(8,128)(2,1)}), bf16[72,4096]{1,0:T(8,128)(2,1)}) %reduce-scatter.5.cloned.1.call-update) | async-done | bytes 589840 | tf_op jit(solution)/shard_map/reduce_scatter | solution.py:102
  460.3 2.1 fusion.16
  (74 shorter events, 5.9 us)
Async XLA Ops:
  7.2 42.4 %copy-start = (bf16[4096,128]{1,0:T(8,128)(2,1)S(1)}, bf16[4096,128]{1,0:T(8,128)(2,1)}, u32[]{:S(2)}) copy-start(bf16[4096,128]{1,0:T(8,128)(2,1)} %param.24) | copy-start | bytes 3145732
  7.2 42.4 %all-gather.3.cloned.1.call-start = ((), (), s32[]{:S(2)}) async-start(), calls=%async_computation.2 | async-start | bytes 5308416 | tf_op jit(solution)/shard_map/all_gather | solution.py:91
  7.3 5.1 %copy-start.7 = (bf16[1088,16,1,128]{3,1,2,0:T(8,128)(2,1)S(1)}, bf16[1088,16,1,128]{3,1,2,0:T(8,128)(2,1)}, u32[]{:S(2)}) copy-start(bf16[1088,16,1,128]{3,1,2,0:T(8,128)(2,1)} %param.22) | copy-start | bytes 13369348
  12.3 2.1 copy-start.13
  12.3 2.1 copy-start.4
  12.3 3.5 copy-start.12
  12.3 4.1 copy-start.2
  14.5 5.8 %copy-start.15 = (s32[576]{0:T(1024)S(1)}, s32[576]{0:T(1024)}, u32[]{:S(2)}) copy-start(s32[576]{0:T(1024)} %param.18) | copy-start | bytes 6916
  14.5 5.9 %copy-start.3 = (s32[65,64]{0,1:T(8,128)S(1)}, s32[65,64]{0,1:T(8,128)}, u32[]{:S(2)}) copy-start(s32[65,64]{0,1:T(8,128)} %param.19) | copy-start | bytes 49924
  15.8 329.0 %reduce-scatter.3.cloned.1.call-start = ((), (), s32[]{:S(2)}) async-start(), calls=%async_computation.3 | async-start | bytes 5308416 | tf_op jit(solution)/shard_map/reduce_scatter | solution.py:95
  53.6 71.5 %copy-start.16 = (bf16[4096,128]{1,0:T(8,128)(2,1)S(1)}, bf16[4096,128]{1,0:T(8,128)(2,1)}, u32[]{:S(2)}) copy-start(bf16[4096,128]{1,0:T(8,128)(2,1)} %param.25) | copy-start | bytes 3145732
  275.0 2.6 copy-start.9
  275.0 2.6 copy-start.10
  299.2 2.5 copy-start.11
  301.7 2.5 copy-start.8
  308.6 0.7 copy-start.14
  308.7 69.8 %all-gather.5.cloned.1.call-start = ((), (), s32[]{:S(2)}) async-start(), calls=%async_computation.4 | async-start | bytes 5308416 | tf_op jit(solution)/shard_map/all_gather | solution.py:97
  348.4 111.9 %reduce-scatter.5.cloned.1.call-start = ((), (), s32[]{:S(2)}) async-start(), calls=%async_computation.5 | async-start | bytes 5308416 | tf_op jit(solution)/shard_map/reduce_scatter | solution.py:102
  393.2 69.3 %copy-start.1 = (bf16[4096,128]{1,0:T(8,128)(2,1)S(1)}, bf16[4096,128]{1,0:T(8,128)(2,1)}, u32[]{:S(2)}) copy-start(bf16[4096,128]{1,0:T(8,128)(2,1)} %param.24) | copy-start | bytes 3145732
  424.1 36.3 %copy-start.5 = (bf16[72,4096]{1,0:T(8,128)(2,1)S(1)}, bf16[72,4096]{1,0:T(8,128)(2,1)}, u32[]{:S(2)}) copy-start(bf16[72,4096]{1,0:T(8,128)(2,1)} %param.16) | copy-start | bytes 1769476
  424.1 36.3 %copy-start.6 = (bf16[72,4096]{1,0:T(8,128)(2,1)S(1)}, bf16[72,4096]{1,0:T(8,128)(2,1)}, u32[]{:S(2)}) copy-start(bf16[72,4096]{1,0:T(8,128)(2,1)} %reduce-scatter.3.cloned.1.call-done) | copy-start | bytes 1769476
Sparse Core Ops, SparseCore 0:
  15.9 33.6 all-gather.2
  308.8 36.0 reduce-scatter.2
  348.6 29.8 all-gather.4
  424.2 36.0 reduce-scatter.4
where the time goes:
time: 472 us; the launch traced here: 469 us
  local copies, waits for them, and re-layouts  229 us (49%)
  waiting for transfers between devices  122 us (26%)
  matrix products  87.9 us (19%)
  between operations  16 us (3%)
  other arithmetic  13.5 us (3%)
    scatter x1, local copies, waits for them, and re-layouts, qkv_cache(): k_cache = k_pages.at[page_ids, slot_ids].set(k_rows)  67 us
    scatter x1, local copies, waits for them, and re-layouts, qkv_cache(): v_cache = v_pages.at[page_ids, slot_ids].set(v_rows)  67 us
    reduce_scatter x1, waiting for transfers between devices, device_layer(): lax.psum_scatter(down_part, 'tp', scatter_dimension=0, tiled=True)  36.2 us
    reduce_scatter x1, waiting for transfers between devices, device_layer(): lax.psum_scatter(attn_part, 'tp', scatter_dimension=0, tiled=True)  35.5 us
    gather x1, local copies, waits for them, and re-layouts, attend(): v_cache[dec_rows].reshape(decode_len, key_span, kv_heads, head_dim)  34.2 us
    gather x1, local copies, waits for them, and re-layouts, attend(): k_cache[dec_rows].reshape(decode_len, key_span, kv_heads, head_dim)  34.2 us
    dot_general x1, matrix products, device_layer(): jnp.dot(act_rows, w_down, preferred_element_type=jnp.float32)  30.9 us
    all_gather x1, waiting for transfers between devices, device_layer(): lax.all_gather(rms_norm(mid_rows, g_mlp), 'tp', axis=0, tiled=True)  29.9 us
  transfers between devices with their start and end apart: 4, of which 4 were waited for; matrix products, arithmetic and copies ran while one was open for 3% of the time, Pallas kernels for 0%

commit v1 on v0

v1 whole, which is shorter than its diff:
```python
import functools

import jax
import jax.numpy as jnp
from jax import lax
from jax.experimental import pallas as pl
from jax.experimental.pallas import tpu as pltpu
from jax.sharding import PartitionSpec as P, NamedSharding

EPS = 1e-5
THETA = 500000.0


def rms_norm(rows, gain):
    rows32 = rows.astype(jnp.float32)
    inv_rms = lax.rsqrt(jnp.mean(rows32 * rows32, axis=-1, keepdims=True) + EPS)
    return (rows32 * inv_rms * gain.astype(jnp.float32)).astype(jnp.bfloat16)


def rotary(vals, positions):
    half_dim = vals.shape[-1] // 2
    inv_freq = THETA ** (-jnp.arange(half_dim, dtype=jnp.float32) * 2.0 / vals.shape[-1])
    angles = positions.astype(jnp.float32)[:, None] * inv_freq[None, :]
    cosine = jnp.cos(angles)[:, None, :]
    sine_val = jnp.sin(angles)[:, None, :]
    vals32 = vals.astype(jnp.float32)
    first_half = vals32[..., :half_dim]
    second_half = vals32[..., half_dim:]
    return jnp.concatenate([first_half * cosine - second_half * sine_val, second_half * cosine + first_half * sine_val], axis=-1).astype(jnp.bfloat16)


ATT_CP = dict(vmem_limit_bytes=60 * 1024 * 1024)
LOG2E = 1.4426950408889634


def attend_kernel(dec_len, heads, dec_pages, tab, req, pos, last, q, k_new, v_new, k_in, v_in, o, k_out, v_out, kc, vc, kg, vg, kch, vch, kf, vf, sems):
    tokens, head_dim = k_new.shape
    page_len = kc.shape[1]
    chunk = tokens - dec_len
    span = kch.shape[0]
    prefix = span - chunk
    pre_pages = prefix // page_len
    scale = head_dim ** -0.5 * LOG2E
    r0 = req[0]

    def pull(j, carry):
        page = tab[j, r0]
        rows = pl.ds(pl.multiple_of(j * page_len, page_len), page_len)
        pltpu.make_async_copy(k_in.at[page], kch.at[rows], sems.at[0]).start()
        pltpu.make_async_copy(v_in.at[page], vch.at[rows], sems.at[1]).start()
        return carry

    lax.fori_loop(0, pre_pages, pull, 0)
    load_k = pltpu.make_async_copy(k_in, kc, sems.at[2])
    load_v = pltpu.make_async_copy(v_in, vc, sems.at[3])
    load_k.start()
    load_v.start()
    kch[prefix:, :] = k_new[:chunk, :]
    vch[prefix:, :] = v_new[:chunk, :]
    kf[...] = k_new[chunk:, :].astype(jnp.float32)
    vf[...] = v_new[chunk:, :].astype(jnp.float32)
    pltpu.make_async_copy(kch.at[pl.ds(0, prefix)], kch.at[pl.ds(0, prefix)], sems.at[0]).wait()
    pltpu.make_async_copy(vch.at[pl.ds(0, prefix)], vch.at[pl.ds(0, prefix)], sems.at[1]).wait()

    def nt(a, b):
        return lax.dot_general(a, b, (((1,), (1,)), ((), ())), preferred_element_type=jnp.float32)

    blk = 128
    for b in range(chunk // blk):
        rows = slice(b * blk, (b + 1) * blk)
        full = prefix + b * blk
        qb = jnp.concatenate([q[rows, h * head_dim:(h + 1) * head_dim] for h in range(heads)], axis=0)
        s1 = nt(qb, kch[:full, :])
        s2 = nt(qb, kch[full:full + blk, :])
        row_id = lax.broadcasted_iota(jnp.int32, s2.shape, 0) % blk
        col_id = lax.broadcasted_iota(jnp.int32, s2.shape, 1)
        s2 = jnp.where(col_id <= row_id, s2, -1e30)
        m = jnp.maximum(jnp.max(s1, axis=1, keepdims=True), jnp.max(s2, axis=1, keepdims=True))
        w1 = jnp.exp2((s1 - m) * scale)
        w2 = jnp.exp2((s2 - m) * scale)
        total = jnp.sum(w1, axis=1, keepdims=True) + jnp.sum(w2, axis=1, keepdims=True)
        mix = jnp.dot(w1.astype(jnp.bfloat16), vch[:full, :], preferred_element_type=jnp.float32)
        mix = mix + jnp.dot(w2.astype(jnp.bfloat16), vch[full:full + blk, :], preferred_element_type=jnp.float32)
        ob = (mix / total).astype(jnp.bfloat16)
        for h in range(heads):
            o[rows, h * head_dim:(h + 1) * head_dim] = ob[h * blk:(h + 1) * blk, :]

    load_k.wait()
    load_v.wait()

    def put_page(j, carry):
        page = tab[pre_pages + j, r0]
        rows = pl.ds(pl.multiple_of(j * page_len, page_len), page_len)
        kc[page] = k_new[rows, :]
        vc[page] = v_new[rows, :]
        return carry

    lax.fori_loop(0, chunk // page_len, put_page, 0)
    slot_id = lax.broadcasted_iota(jnp.int32, (page_len, head_dim), 0)

    def put_row(r, carry):
        p = pos[chunk + r]
        page = tab[p // page_len, req[chunk + r]]
        here = slot_id == p % page_len
        kc[page] = jnp.where(here, kf[pl.ds(r, 1), :], kc[page].astype(jnp.float32)).astype(jnp.bfloat16)
        vc[page] = jnp.where(here, vf[pl.ds(r, 1), :], vc[page].astype(jnp.float32)).astype(jnp.bfloat16)
        return carry

    lax.fori_loop(0, dec_len, put_row, 0)
    store_k = pltpu.make_async_copy(kc, k_out, sems.at[2])
    store_v = pltpu.make_async_copy(vc, v_out, sems.at[3])
    store_k.start()
    store_v.start()

    def take(r, carry):
        rid = req[chunk + r]
        for j in range(dec_pages):
            page = tab[j, rid]
            rows = pl.ds(pl.multiple_of((r * dec_pages + j) * page_len, page_len), page_len)
            kg[rows, :] = kc[page]
            vg[rows, :] = vc[page]
        return carry

    lax.fori_loop(0, dec_len, take, 0)
    grp = 16
    dspan = dec_pages * page_len
    for g in range(dec_len // grp):
        rows = slice(chunk + g * grp, chunk + (g + 1) * grp)
        keys = slice(g * grp * dspan, (g + 1) * grp * dspan)
        qb = jnp.concatenate([q[rows, h * head_dim:(h + 1) * head_dim] for h in range(heads)], axis=0)
        s = nt(qb, kg[keys, :])
        lg = last[g * grp:(g + 1) * grp, :]
        low = (lax.broadcasted_iota(jnp.int32, (grp * heads, 1), 0) % grp) * dspan
        high = low + jnp.concatenate([lg] * heads, axis=0)
        col = lax.broadcasted_iota(jnp.int32, s.shape, 1)
        s = jnp.where((col >= low) & (col <= high), s, -1e30)
        m = jnp.max(s, axis=1, keepdims=True)
        w = jnp.exp2((s - m) * scale)
        total = jnp.sum(w, axis=1, keepdims=True)
        mix = jnp.dot(w.astype(jnp.bfloat16), vg[keys, :], preferred_element_type=jnp.float32)
        ob = (mix / total).astype(jnp.bfloat16)
        for h in range(heads):
            o[rows, h * head_dim:(h + 1) * head_dim] = ob[h * grp:(h + 1) * grp, :]
    store_k.wait()
    store_v.wait()


DEC_SPAN = 256


def attend(q, k_new, v_new, positions, req_ids, block_table, ctx_len, k_pages, v_pages):
    tokens, head_dim = k_new.shape
    pages, page_len = k_pages.shape[:2]
    dec_len = block_table.shape[0] - 1
    chunk = tokens - dec_len
    heads = q.shape[1] // head_dim
    span = block_table.shape[1] * page_len
    dec_pages = DEC_SPAN // page_len
    last = jnp.minimum(positions[chunk:], ctx_len[req_ids[chunk:]] - 1)[:, None]
    smem = pl.BlockSpec(memory_space=pltpu.SMEM)
    vmem = pl.BlockSpec(memory_space=pltpu.VMEM)
    hbm = pl.BlockSpec(memory_space=pl.ANY)
    cache = jax.ShapeDtypeStruct((pages, page_len, head_dim), jnp.bfloat16)
    o, k_out, v_out = pl.pallas_call(
        functools.partial(attend_kernel, dec_len, heads, dec_pages),
        out_shape=(jax.ShapeDtypeStruct(q.shape, jnp.bfloat16), cache, cache),
        in_specs=[smem, smem, smem, vmem, vmem, vmem, vmem, hbm, hbm],
        out_specs=(vmem, hbm, hbm),
        scratch_shapes=[
            pltpu.VMEM((pages, page_len, head_dim), jnp.bfloat16),
            pltpu.VMEM((pages, page_len, head_dim), jnp.bfloat16),
            pltpu.VMEM((dec_len * DEC_SPAN, head_dim), jnp.bfloat16),
            pltpu.VMEM((dec_len * DEC_SPAN, head_dim), jnp.bfloat16),
            pltpu.VMEM((span, head_dim), jnp.bfloat16),
            pltpu.VMEM((span, head_dim), jnp.bfloat16),
            pltpu.VMEM((dec_len, head_dim), jnp.float32),
            pltpu.VMEM((dec_len, head_dim), jnp.float32),
            pltpu.SemaphoreType.DMA((4,)),
        ],
        compiler_params=pltpu.CompilerParams(**ATT_CP),
        name="attend",
    )(block_table.T, req_ids, positions, last, q, k_new, v_new, k_pages.reshape(cache.shape), v_pages.reshape(cache.shape))
    return o, k_out.reshape(k_pages.shape), v_out.reshape(v_pages.shape)


def project(hidden, positions, head_dim, w_q, w_k, w_v):
    tokens = hidden.shape[0]
    q_rows = jnp.dot(hidden, w_q, preferred_element_type=jnp.float32).astype(jnp.bfloat16).reshape(tokens, -1, head_dim)
    k_rows = jnp.dot(hidden, w_k, preferred_element_type=jnp.float32).astype(jnp.bfloat16).reshape(tokens, -1, head_dim)
    v_rows = jnp.dot(hidden, w_v, preferred_element_type=jnp.float32).astype(jnp.bfloat16)
    return rotary(q_rows, positions).reshape(tokens, -1), rotary(k_rows, positions).reshape(tokens, -1), v_rows


def solution(mesh):
    row_spec = P(('dp', 'tp'), None)
    group_vec = P('dp')
    table_spec = P('dp', None)
    cache_spec = P('dp', None, 'tp', None)
    col_split = P(None, 'tp')
    row_split = P('tp', None)
    gain_spec = P(None)

    def device_layer(x_in, req_ids, positions, block_table, ctx_len, k_pages, v_pages, w_q, w_k, w_v, w_o, w_gate, w_up, w_down, g_attn, g_mlp):
        hidden = lax.all_gather(rms_norm(x_in, g_attn), 'tp', axis=0, tiled=True)
        q_rows, k_rows, v_rows = project(hidden, positions, k_pages.shape[3], w_q, w_k, w_v)
        attn_rows, k_cache, v_cache = attend(q_rows, k_rows, v_rows, positions, req_ids, block_table, ctx_len, k_pages, v_pages)
        attn_part = jnp.dot(attn_rows, w_o, preferred_element_type=jnp.float32).astype(jnp.bfloat16)
        attn_sum = lax.psum_scatter(attn_part, 'tp', scatter_dimension=0, tiled=True)
        mid_rows = (x_in.astype(jnp.float32) + attn_sum.astype(jnp.float32)).astype(jnp.bfloat16)
        hidden_mlp = lax.all_gather(rms_norm(mid_rows, g_mlp), 'tp', axis=0, tiled=True)
        gate_proj = jnp.dot(hidden_mlp, w_gate, preferred_element_type=jnp.float32)
        up_proj = jnp.dot(hidden_mlp, w_up, preferred_element_type=jnp.float32)
        act_rows = (jax.nn.silu(gate_proj) * up_proj).astype(jnp.bfloat16)
        down_part = jnp.dot(act_rows, w_down, preferred_element_type=jnp.float32).astype(jnp.bfloat16)
        down_sum = lax.psum_scatter(down_part, 'tp', scatter_dimension=0, tiled=True)
        x_out = (mid_rows.astype(jnp.float32) + down_sum.astype(jnp.float32)).astype(jnp.bfloat16)
        return x_out, k_cache, v_cache

    return jax.shard_map(device_layer, mesh=mesh, in_specs=(row_spec, group_vec, group_vec, table_spec, group_vec, cache_spec, cache_spec, col_split, col_split, col_split, row_split, col_split, col_split, row_split, gain_spec, gain_spec), out_specs=(row_spec, cache_spec, cache_spec), check_vma=False)
```

time: 472 us -> 249 us (0.53)
  local copies, waits for them, and re-layouts: 229 us -> 5.31 us
  matrix products: 87.9 us -> 65.9 us
  Pallas kernels: 0 us -> 15.6 us
  waiting for transfers between devices: 122 us -> 130 us
    scatter x2 -> x0, local copies, waits for them, and re-layouts: 134 us -> none  [the longest x1 67 us: qkv_cache(): k_cache = k_pages.at[page_ids, slot_ids].set(k_rows)]
    gather x7 -> x1, local copies, waits for them, and re-layouts: 84 us -> 1.43 us  [attend(): last = jnp.minimum(positions[chunk:], ctx_len[req_ids[chunk:]] - 1)[:, None]]
    dot_general x7 -> x3, matrix products: 37.9 us -> 13.1 us  [the longest x1 7.23 us: project(): jnp.dot(hidden, w_q, preferred_element_type=jnp.float32)]
    pallas_call x0 -> x1, Pallas kernels: none -> 15.6 us  [attend(): pl.pallas_call(functools.partial(attend_kernel, dec_len, heads, dec_pages...]
    all_gather x1, waiting for transfers between devices: 19.8 us -> 28.3 us  [device_layer(): hidden = lax.all_gather(rms_norm(x_in, g_attn), 'tp', axis=0, tiled=True)]
    unnamed x37 -> x19, local copies, waits for them, and re-layouts: 7.67 us -> 1.51 us
  transfers between devices with their start and end apart: 4 -> 4, of which waited for: 4 -> 4; matrix products, arithmetic and copies ran while one was open for 3% -> 2% of each run, Pallas kernels for 0% -> 0%
where the time goes in v1:
time: 249 us; the launch traced here: 248 us
  waiting for transfers between devices  130 us (52%)
  matrix products  65.9 us (26%)
  other arithmetic  16.8 us (7%)
  Pallas kernels  15.6 us (6%)
  between operations  13.9 us (6%)
  local copies, waits for them, and re-layouts  5.31 us (2%)
    reduce_scatter x1, waiting for transfers between devices, device_layer(): lax.psum_scatter(down_part, 'tp', scatter_dimension=0, tiled=True)  36.2 us
    reduce_scatter x1, waiting for transfers between devices, device_layer(): lax.psum_scatter(attn_part, 'tp', scatter_dimension=0, tiled=True)  35.6 us
    dot_general x1, matrix products, device_layer(): jnp.dot(act_rows, w_down, preferred_element_type=jnp.float32)  30.9 us
    all_gather x1, waiting for transfers between devices, device_layer(): lax.all_gather(rms_norm(mid_rows, g_mlp), 'tp', axis=0, tiled=True)  29.9 us
    all_gather x1, waiting for transfers between devices, device_layer(): hidden = lax.all_gather(rms_norm(x_in, g_attn), 'tp', axis=0, tiled=True)  28.3 us
    pallas_call x1, Pallas kernels, attend(): pl.pallas_call(functools.partial(attend_kernel, dec_len, heads, dec_pages...  15.6 us
    dot_general x1, matrix products, device_layer(): gate_proj = jnp.dot(hidden_mlp, w_gate, preferred_element_type=jnp.float32)  14.7 us
    dot_general x1, matrix products, project(): jnp.dot(hidden, w_q, preferred_element_type=jnp.float32)  7.23 us
  transfers between devices with their start and end apart: 4, of which 4 were waited for; matrix products, arithmetic and copies ran while one was open for 2% of the time, Pallas kernels for 0%

profile of v1, /device:TPU:80, one launch (start us, length us, event | category | flops | bytes accessed | tf_op | source)
XLA Modules:
  0.0 248.0 jit_solution(684838378716475269)
XLA Ops:
  7.3 1.4 fusion.2
  8.6 0.7 convert_element_type.76
  9.3 2.1 fusion.4
  11.6 0.7 convert_element_type.81
  12.3 0.7 compare_select_fusion
  13.0 1.4 gather_fusion
  14.4 0.7 minimum_bitcast_fusion
  15.1 0.7 copy.22.last
  15.8 1.1 multiply_cosine_fusion.1
  16.9 28.3 %all-gather.3.cloned.1.call-done = bf16[576,4096]{1,0:T(8,128)(2,1)} async-done(((bf16[72,4096]{1,0:T(8,128)(2,1)}), bf16[576,4096]{1,0:T(8,128)(2,1)}) %all-gather.3.cloned.1.call-update) | async-done | bytes 4718608 | tf_op jit(solution)/shard_map/all_gather | solution.py:204
  45.2 7.2 %fusion.1 = f32[576,512]{1,0:T(8,128)} fusion(bf16[576,4096]{1,0:T(8,128)(2,1)} %all-gather.3.cloned.1.call-done, bf16[4096,512]{1,0:T(8,128)(2,1)} %param.23), kind=kOutput, calls=%fused_computation.12 | convolution fusion | flops 2416508928 | bytes 10092544 | tf_op jit(solution)/shard_map/dot_general | solution.py:188
  52.5 1.7 reshape.160
  54.2 3.9 %fusion.11 = f32[576,1,128]{2,0,1:T(8,128)S(1)} fusion(bf16[576,4096]{1,0:T(8,128)(2,1)} %all-gather.3.cloned.1.call-done, bf16[4096,128]{1,0:T(8,128)(2,1)S(1)} %copy-done), kind=kOutput, calls=%fused_computation.26 | convolution fusion | flops 604127232 | bytes 6062080 | tf_op jit(solution)/shard_map/dot_general | solution.py:189
  58.1 1.4 fusion.21
  59.4 1.0 subtract_convert_fusion
  60.4 0.8 pad_maximum_fusion
  61.2 0.9 copy.27
  62.1 0.8 pad_maximum_fusion.1.k_new
  62.9 2.0 convolution_convert_fusion.3.v_new
  64.9 15.6 %attend.1 = (bf16[576,512]{1,0:T(8,128)(2,1)}, bf16[1088,16,128]{2,1,0:T(8,128)(2,1)}, bf16[1088,16,128]{2,1,0:T(8,128)(2,1)}) custom-call(s32[64,65]{1,0:T(8,128)} %bitcast.41, s32[576]{0:T(1024)} %req.1, s32[576]{0:T(1024)} %pos.1, s32[64,1]{1,0:T(8,128)} %copy.22.last, bf16[576,512]{1,0:T(8,128)(2,1)} %bitcast.39, ...), custom_call_target="tpu_custom_call" | custom-call | tf_op jit(solution)/shard_map/attend/pallas_call | solution.py:164
  80.5 7.1 %convolution_convert_fusion = bf16[576,4096]{1,0:T(8,128)(2,1)} fusion(bf16[576,512]{1,0:T(8,128)(2,1)} %get-tuple-element.6, bf16[512,4096]{1,0:T(8,128)(2,1)} %param.26), kind=kOutput, calls=%fused_computation.1 | convolution fusion | flops 2418278400 | bytes 9502720 | tf_op jit(solution)/shard_map/dot_general | solution.py:207
  87.7 0.1 all-gather.5.cloned.1.call-start
  87.8 0.6 copy-done.5
  88.3 35.6 %reduce-scatter.3.cloned.1.call-done = bf16[72,4096]{1,0:T(8,128)(2,1)} async-done(((bf16[576,4096]{1,0:T(8,128)(2,1)}), bf16[72,4096]{1,0:T(8,128)(2,1)}) %reduce-scatter.3.cloned.1.call-update) | async-done | bytes 589840 | tf_op jit(solution)/shard_map/reduce_scatter | solution.py:208
  123.9 1.4 fusion.6
  125.3 2.1 fusion.8
  127.5 0.1 reduce-scatter.5.cloned.1.call-start
  127.5 29.9 %all-gather.5.cloned.1.call-done = bf16[576,4096]{1,0:T(8,128)(2,1)} async-done(((bf16[72,4096]{1,0:T(8,128)(2,1)}), bf16[576,4096]{1,0:T(8,128)(2,1)}) %all-gather.5.cloned.1.call-update) | async-done | bytes 4718608 | tf_op jit(solution)/shard_map/all_gather | solution.py:210
  157.5 14.7 %fusion.23 = f32[576,1792]{1,0:T(8,128)} fusion(bf16[576,4096]{1,0:T(8,128)(2,1)} %all-gather.5.cloned.1.call-done, bf16[4096,1792]{1,0:T(8,128)(2,1)} %param.27), kind=kOutput, calls=%fused_computation.51 | convolution fusion | flops 8455716864 | bytes 23527424 | tf_op jit(solution)/shard_map/dot_general | solution.py:211
  172.2 30.9 %convolution_convert_fusion.1 = bf16[576,4096]{1,0:T(8,128)(2,1)} fusion(bf16[1792,4096]{1,0:T(8,128)(2,1)} %param.29, f32[576,1792]{1,0:T(8,128)} %fusion.23, bf16[576,4096]{1,0:T(8,128)(2,1)} %all-gather.5.cloned.1.call-done, bf16[4096,1792]{1,0:T(8,128)(2,1)} %param.28), kind=kOutput, calls=%fused_computation.2 | convolution fusion | flops 16919986176 | bytes 42926080 | tf_op jit(solution)/shard_map/dot_general | solution.py:214
  203.2 36.2 %reduce-scatter.5.cloned.1.call-done = bf16[72,4096]{1,0:T(8,128)(2,1)} async-done(((bf16[576,4096]{1,0:T(8,128)(2,1)}), bf16[72,4096]{1,0:T(8,128)(2,1)}) %reduce-scatter.5.cloned.1.call-update) | async-done | bytes 589840 | tf_op jit(solution)/shard_map/reduce_scatter | solution.py:215
  239.4 2.1 fusion.9
  (29 shorter events, 0.4 us)
Async XLA Ops:
  7.2 47.0 %copy-start = (bf16[4096,128]{1,0:T(8,128)(2,1)S(1)}, bf16[4096,128]{1,0:T(8,128)(2,1)}, u32[]{:S(2)}) copy-start(bf16[4096,128]{1,0:T(8,128)(2,1)} %param.24) | copy-start | bytes 3145732
  7.2 38.0 %all-gather.3.cloned.1.call-start = ((), (), s32[]{:S(2)}) async-start(), calls=%async_computation.2 | async-start | bytes 5308416 | tf_op jit(solution)/shard_map/all_gather | solution.py:204
  11.5 112.4 %reduce-scatter.3.cloned.1.call-start = ((), (), s32[]{:S(2)}) async-start(), calls=%async_computation.3 | async-start | bytes 5308416 | tf_op jit(solution)/shard_map/reduce_scatter | solution.py:208
  54.1 8.7 %slice-start = ((s8[4718592]{0:T(1024)(128)(4,1)}), s8[4194304]{0:T(1024)(128)(4,1)S(1)}, s32[]{:S(2)}) async-start(s8[4718592]{0:T(1024)(128)(4,1)} %bitcast.42), calls=%async_computation.6 | async-start | bytes 8388608
  58.0 4.9 %slice-start.1 = ((s8[4718592]{0:T(1024)(128)(4,1)}), s8[524288]{0:T(1024)(128)(4,1)S(1)}, s32[]{:S(2)}) async-start(s8[4718592]{0:T(1024)(128)(4,1)} %bitcast.42), calls=%async_computation.7 | async-start | bytes 1048576
  58.0 4.9 %copy-start.6 = (bf16[4096,128]{1,0:T(8,128)(2,1)S(1)}, bf16[4096,128]{1,0:T(8,128)(2,1)}, u32[]{:S(2)}) copy-start(bf16[4096,128]{1,0:T(8,128)(2,1)} %param.25) | copy-start | bytes 3145732
  87.6 0.7 copy-start.5
  87.7 36.3 %copy-start.2 = (bf16[72,4096]{1,0:T(8,128)(2,1)S(1)}, bf16[72,4096]{1,0:T(8,128)(2,1)}, u32[]{:S(2)}) copy-start(bf16[72,4096]{1,0:T(8,128)(2,1)} %param.16) | copy-start | bytes 1769476
  87.7 69.8 %all-gather.5.cloned.1.call-start = ((), (), s32[]{:S(2)}) async-start(), calls=%async_computation.4 | async-start | bytes 5308416 | tf_op jit(solution)/shard_map/all_gather | solution.py:210
  127.5 111.9 %reduce-scatter.5.cloned.1.call-start = ((), (), s32[]{:S(2)}) async-start(), calls=%async_computation.5 | async-start | bytes 5308416 | tf_op jit(solution)/shard_map/reduce_scatter | solution.py:215
  172.2 69.3 %copy-start.1 = (bf16[4096,128]{1,0:T(8,128)(2,1)S(1)}, bf16[4096,128]{1,0:T(8,128)(2,1)}, u32[]{:S(2)}) copy-start(bf16[4096,128]{1,0:T(8,128)(2,1)} %param.24) | copy-start | bytes 3145732
  203.1 36.3 %copy-start.3 = (bf16[72,4096]{1,0:T(8,128)(2,1)S(1)}, bf16[72,4096]{1,0:T(8,128)(2,1)}, u32[]{:S(2)}) copy-start(bf16[72,4096]{1,0:T(8,128)(2,1)} %param.16) | copy-start | bytes 1769476
  203.1 36.3 %copy-start.4 = (bf16[72,4096]{1,0:T(8,128)(2,1)S(1)}, bf16[72,4096]{1,0:T(8,128)(2,1)}, u32[]{:S(2)}) copy-start(bf16[72,4096]{1,0:T(8,128)(2,1)} %reduce-scatter.3.cloned.1.call-done) | copy-start | bytes 1769476
Sparse Core Ops, SparseCore 0:
  11.6 33.5 all-gather.2
  87.8 36.0 reduce-scatter.2
  127.6 29.8 all-gather.4
  203.3 36.0 reduce-scatter.4
